TPU v7x, 32 devices: a whole 2x2x4 slice. The times are simulated.
32 devices in a mesh: dp: 4 (over y, x), expert: 8 (over z, core).
Axes of the slice: x: 2, y: 2, z: 4, core: 2. Of those that a mesh axis runs over, the one named last changes fastest.
Arguments:
- tokens: bfloat16 [1024, 4096], P('dp', 'expert'), may hold values from -6 to 6
- routing: int32 [1024, 2], P('dp'), may hold values from 0 to 3, all different within a row; in each aligned block of 256 rows (0 to 255, 256 to 511, ...) at most 192 rows name the same one
- gate_weight: bfloat16 [4096, 4], P('expert'), may hold values from -0.09375 to 0.09375
- expert_in: bfloat16 [4, 4096, 8192], P('dp', None, 'expert'), may hold values from -0.09375 to 0.09375
- expert_out: bfloat16 [4, 8192, 4096], P('dp', 'expert'), may hold values from -0.75 to 0.75
Outputs:
- mixed: bfloat16 [1024, 4096], P('dp', 'expert')
Inputs may be any that keep to these rules, and one draw needn't show every extreme that they name: `routing`: each row names two different experts. Within the 256 rows of one group, no expert is named by more than 192 rows, a bound that some block reaches.
All inputs are finite; a program needn't handle non-finite values.
Results may differ from a plain program's by a relative error of at most 0.02.
Values may be sent and summed in bfloat16 or wider, within the bound.
A program may use at most 64 MiB of HBM per device.

v0:
```python
import jax
import jax.numpy as jnp
from jax import lax
from jax.sharding import PartitionSpec as P


def softmax_rows(logits):
    raised = jnp.exp(logits)
    return raised / jnp.sum(raised, axis=-1, keepdims=True)


def pick_chosen(softmax_all, picks):
    experts = softmax_all.shape[1]
    labels = lax.broadcasted_iota(jnp.int32, (picks.shape[0], 2, experts), 2)
    selected = labels == picks[:, :, None]
    return jnp.sum(jnp.where(selected, softmax_all[:, None, :], 0.0), axis=-1).astype(jnp.bfloat16)


def expert_rows(block_rows, weight_in, weight_out):
    sources = block_rows.shape[0]
    slots_here = block_rows.shape[1]
    width_local = block_rows.shape[2]
    flat_rows = block_rows.reshape(sources * slots_here, width_local)
    pre_act = jnp.dot(
        lax.all_gather(flat_rows, "expert", axis=1, tiled=True),
        weight_in,
        preferred_element_type=jnp.float32,
    )
    hidden = jax.nn.gelu(pre_act, approximate=True).astype(jnp.bfloat16)
    partial_out = jnp.dot(hidden, weight_out, preferred_element_type=jnp.float32)
    summed = lax.psum_scatter(
        partial_out.astype(jnp.bfloat16), "expert", scatter_dimension=1, tiled=True
    )
    return summed.reshape(sources, slots_here, width_local)


def shards(tokens, routing, gate_weight, expert_in, expert_out):
    group_size = tokens.shape[0]
    width_local = tokens.shape[1]
    experts = gate_weight.shape[1]
    dp_count = lax.axis_size("dp")
    capacity = 3 * group_size // dp_count
    weight_in = expert_in[0]
    weight_out = expert_out[0]
    partial_logits = jnp.dot(tokens, gate_weight, preferred_element_type=jnp.float32)
    logits = lax.psum(partial_logits, "expert")
    chosen = pick_chosen(softmax_rows(logits), routing)
    order = jnp.concatenate([routing[:, 0], routing[:, 1]], axis=0)
    labels = lax.broadcasted_iota(jnp.int32, (2 * group_size, experts), 1)
    onehot = (labels == order[:, None]).astype(jnp.int32)
    before = jnp.cumsum(onehot, axis=0) - onehot
    slot_flat = jnp.sum(before * onehot, axis=1)
    slot_index = jnp.stack([slot_flat[:group_size], slot_flat[group_size:]], axis=1)
    target = routing * capacity + slot_index
    columns = lax.broadcasted_iota(jnp.int32, (group_size, experts * capacity), 1)
    first_hit = columns == target[:, 0:1]
    second_hit = columns == target[:, 1:2]
    assign = jnp.logical_or(first_hit, second_hit).astype(jnp.bfloat16)
    outgoing = jnp.einsum("gs,gd->sd", assign, tokens, preferred_element_type=jnp.float32)
    outgoing = outgoing.astype(jnp.bfloat16).reshape(experts, capacity, width_local)
    incoming = lax.all_to_all(outgoing, "dp", split_axis=0, concat_axis=0, tiled=True)
    processed = expert_rows(incoming, weight_in, weight_out)
    returned_rows = lax.all_to_all(processed, "dp", split_axis=0, concat_axis=0, tiled=True)
    zero_weight = jnp.zeros((), jnp.bfloat16)
    combine = jnp.where(first_hit, chosen[:, 0:1], zero_weight) + jnp.where(
        second_hit, chosen[:, 1:2], zero_weight
    )
    mixed = jnp.dot(
        combine,
        returned_rows.reshape(experts * capacity, width_local),
        preferred_element_type=jnp.float32,
    )
    return mixed.astype(jnp.bfloat16)


def solution(mesh):
    placed = (
        P("dp", "expert"),
        P("dp", None),
        P("expert", None),
        P("dp", None, "expert"),
        P("dp", "expert", None),
    )
    return jax.shard_map(
        shards, mesh=mesh, in_specs=placed, out_specs=P("dp", "expert"), check_vma=False
    )
```

profile of v0, /device:TPU:0, one launch (start us, length us, event | category | flops | bytes accessed | tf_op | source)
XLA Modules:
  0.0 207.8 jit_solution(6517261389319682265)
XLA Ops:
  6.5 0.0 copy-start
  6.5 0.0 all-gather.2.cloned.1.call-start
  6.5 0.8 fusion.45
  7.3 1.2 reduce-window.6
  8.5 0.2 slice_reduce_fusion
  8.8 0.2 reduce-window.9
  8.9 0.1 add_bitcast_fusion
  9.1 0.7 add_add_fusion
  9.8 0.0 copy-done
  9.8 0.6 convolution_convert_fusion
  10.3 16.4 %all_to_all.10 = bf16[4,192,512]{2,1,0:T(8,128)(2,1)} all-to-all(bf16[4,192,512]{2,1,0:T(8,128)(2,1)S(1)} %bitcast.51), channel_id=1, replica_groups=mesh['dp'=4,'expert'=8] {'dp'}, dimensions={0} | all-to-all | bytes 1572864 | tf_op jit(solution)/shard_map/all_to_all | solution.py:61
  26.8 0.0 all-gather.2.cloned.1.call-update
  26.8 0.0 reduce-scatter.2.cloned.1.call-start
  26.9 64.5 %all-gather.2.cloned.1.call-done = bf16[768,4096]{1,0:T(8,128)(2,1)} async-done(((bf16[768,512]{1,0:T(8,128)(2,1)}), bf16[768,4096]{1,0:T(8,128)(2,1)}) %all-gather.2.cloned.1.call-update) | async-done | bytes 6291472 | tf_op jit(solution)/shard_map/all_gather | solution.py:25
  91.4 22.3 %fusion.4 = bf16[768,4096]{1,0:T(8,128)(2,1)} fusion(bf16[1,1024,4096]{2,1,0:T(8,128)(2,1)} %param.9, bf16[768,4096]{1,0:T(8,128)(2,1)} %all-gather.2.cloned.1.call-done, bf16[1,4096,1024]{2,1,0:T(8,128)(2,1)} %param.8), kind=kOutput, calls=%fused_computation.4 | convolution fusion | flops 12895125504 | bytes 29360128 | tf_op jit(solution)/shard_map/dot_general | solution.py:30
  113.6 0.0 reduce-scatter.2.cloned.1.call-update
  113.7 68.5 %reduce-scatter.2.cloned.1.call-done = bf16[768,512]{1,0:T(8,128)(2,1)} async-done(((bf16[768,4096]{1,0:T(8,128)(2,1)}), bf16[768,512]{1,0:T(8,128)(2,1)}) %reduce-scatter.2.cloned.1.call-update) | async-done | bytes 786448 | tf_op jit(solution)/shard_map/reduce_scatter | solution.py:31
  182.2 3.6 %all-to-all-start.1 = ((bf16[4,192,512]{2,1,0:T(8,128)(2,1)}), bf16[4,192,512]{2,1,0:T(8,128)(2,1)S(1)}, u32[]{:S(2)}, u32[]{:S(2)}) async-start(bf16[4,192,512]{2,1,0:T(8,128)(2,1)} %bitcast.49), calls=%async_computation.2 | async-start | bytes 1572864 | tf_op jit(solution)/shard_map/all_to_all | solution.py:63
  185.8 0.0 copy-done.2
  185.8 0.1 fusion.46
  186.0 13.6 %psum.7 = f32[256,4]{0,1:T(4,128)S(1)} all-reduce(f32[256,4]{0,1:T(4,128)S(1)} %fusion.46), channel_id=1, replica_groups=mesh['dp'=4,'expert'=8] {'expert'}, use_global_device_ids=true, to_apply=%region_3.4 | all-reduce | flops 1024 | bytes 8192 | tf_op jit(solution)/shard_map/psum | solution.py:46
  199.6 0.0 copy-done.1
  199.7 0.0 all-to-all-done.1
  199.7 1.2 convolution_convert_fusion.1
  (12 shorter events, 0.1 us)
Async XLA Ops:
  6.5 3.2 %copy-start = (bf16[256,512]{1,0:T(8,128)(2,1)S(1)}, bf16[256,512]{1,0:T(8,128)(2,1)}, u32[]{:S(2)}) copy-start(bf16[256,512]{1,0:T(8,128)(2,1)} %param.5) | copy-start | bytes 786436
  6.5 84.8 %all-gather.2.cloned.1.call-start = ((), (), s32[]{:S(2)}) async-start(), calls=%async_computation.3 | async-start | bytes 7077888 | tf_op jit(solution)/shard_map/all_gather | solution.py:25
  26.8 155.4 %reduce-scatter.2.cloned.1.call-start = ((), (), s32[]{:S(2)}) async-start(), calls=%async_computation.4 | async-start | bytes 7077888 | tf_op jit(solution)/shard_map/reduce_scatter | solution.py:31
  113.6 72.2 %copy-start.2 = (bf16[512,4]{0,1:T(4,128)(2,1)S(1)}, bf16[512,4]{0,1:T(4,128)(2,1)}, u32[]{:S(2)}) copy-start(bf16[512,4]{0,1:T(4,128)(2,1)} %param.7) | copy-start | bytes 12292
  113.6 86.0 %copy-start.1 = (s32[256,2]{0,1:T(2,128)S(1)}, s32[256,2]{0,1:T(2,128)}, u32[]{:S(2)}) copy-start(s32[256,2]{0,1:T(2,128)} %param.6) | copy-start | bytes 6148
  182.2 17.5 %all-to-all-start.1 = ((bf16[4,192,512]{2,1,0:T(8,128)(2,1)}), bf16[4,192,512]{2,1,0:T(8,128)(2,1)S(1)}, u32[]{:S(2)}, u32[]{:S(2)}) async-start(bf16[4,192,512]{2,1,0:T(8,128)(2,1)} %bitcast.49), calls=%async_computation.2 | async-start | bytes 1572864 | tf_op jit(solution)/shard_map/all_to_all | solution.py:63
Sparse Core Ops, SparseCore 0:
  26.9 64.3 all-gather.1
  113.8 68.3 reduce-scatter.1
where the time goes:
time: 208 us
  waiting for transfers between devices  133 us (64%)
  blocking collectives  30 us (14%)
  matrix products  24.2 us (12%)
  between operations  13.5 us (6%)
  starting transfers between devices  3.69 us (2%)
  other arithmetic  2.28 us (1%)
    reduce_scatter x1, waiting for transfers between devices, expert_rows(): lax.psum_scatter(partial_out.astype(jnp.bfloat16), 'expert', scatter_dime...  68.5 us
    all_gather x1, waiting for transfers between devices, expert_rows(): lax.all_gather(flat_rows, 'expert', axis=1, tiled=True)  64.5 us
    dot_general x1, matrix products, expert_rows(): jnp.dot(hidden, weight_out, preferred_element_type=jnp.float32)  22.3 us
    all_to_all x1, blocking collectives, shards(): lax.all_to_all(outgoing, 'dp', split_axis=0, concat_axis=0, tiled=True)  16.4 us
    psum x1, blocking collectives, shards(): logits = lax.psum(partial_logits, 'expert')  13.6 us
  transfers between devices with their start and end apart: 3, of which 2 were waited for; matrix products, arithmetic and copies ran while one was open for 0% of the time, Pallas kernels for 0%

commit v1 on v0

--- a/solution.py
+++ b/solution.py
@@ -1,6 +1,10 @@
+import functools
+
 import jax
 import jax.numpy as jnp
 from jax import lax
+from jax.experimental import pallas as pl
+from jax.experimental.pallas import tpu as pltpu
 from jax.sharding import PartitionSpec as P
 
 
@@ -34,7 +38,7 @@
     return summed.reshape(sources, slots_here, width_local)
 
 
-def shards(tokens, routing, gate_weight, expert_in, expert_out):
+def slots_plan(tokens, routing, gate_weight, expert_in, expert_out):
     group_size = tokens.shape[0]
     width_local = tokens.shape[1]
     experts = gate_weight.shape[1]
@@ -73,6 +77,253 @@
     return mixed.astype(jnp.bfloat16)
 
 
+MESH = pl.DeviceIdType.MESH
+F32 = jnp.float32
+BF16 = jnp.bfloat16
+
+
+def whole_kernel(
+    experts,
+    tok, extra, win_hbm, wout_hbm, out,
+    xs, ex, win, wout, pre, logit, hidden, give, take, part, hop, zin,
+    wsem, xs_s, xs_r, zs, zr, fs, fr, ds, dr, es, er, ps, pr, hs, hr, us, ur,
+):
+    dp, me = lax.axis_index("dp"), lax.axis_index("expert")
+    z, k = me // 2, me % 2
+    depth = lax.axis_size("expert") // 2
+    group, width = tok.shape
+    half = group // 2
+    gx, gy = dp // 2 * 2 + 1 - dp % 2, (1 - dp // 2) * 2 + dp % 2
+    gd = 3 - dp
+    other = z * 2 + 1 - k
+    top, low = pl.ds(0, half), pl.ds(half, half)
+    peers = [(g, me) for g in (gx, gy, gd)]
+    peers += [(dp, lax.rem(me + i, 2 * depth)) for i in range(1, 2 * depth)]
+
+    def send(src, dst, s_sem, r_sem, who):
+        copy = pltpu.make_async_remote_copy(src, dst, s_sem, r_sem, device_id=who, device_id_type=MESH)
+        copy.start()
+        started.append(copy)
+
+    def got(ref, s_sem, r_sem):
+        pltpu.make_async_remote_copy(ref, ref, s_sem, r_sem, device_id=(dp, other), device_id_type=MESH).wait_recv()
+
+    started = []
+    load_in = pltpu.make_async_copy(win_hbm.at[0], win, wsem.at[0])
+    load_out = pltpu.make_async_copy(wout_hbm.at[0], wout, wsem.at[1])
+    load_in.start()
+    load_out.start()
+    barrier = pltpu.get_barrier_semaphore()
+    for who in peers:
+        pl.semaphore_signal(barrier, inc=1, device_id=who, device_id_type=MESH)
+    pl.semaphore_wait(barrier, len(peers))
+
+    def origin(s):
+        return lax.rem(z + depth - s, depth)
+
+    def spread(s):
+        zz = origin(s)
+        block = tok if s == 0 else xs.at[dp, zz, k]
+        for i, (who, rows) in enumerate(((gx, top), (gy, low), (gx, low), (gy, top))):
+            send(block.at[rows], xs.at[dp, zz, k, rows], xs_s.at[s, i], xs_r.at[s, i], (who, me))
+        send(block, xs.at[dp, zz, k], ds.at[s, 0], dr.at[s, 0], (dp, other))
+
+    for i in range(1, depth):
+        send(tok, xs.at[dp, z, k], zs.at[i], zr.at[i], (dp, lax.rem(z + i, depth) * 2 + k))
+    spread(0)
+    for i, who in enumerate(peers):
+        slot = dp if i < 3 else 4 + i - 3
+        send(extra, ex.at[slot], es.at[i], er.at[i], who)
+    xs[dp, z, k] = tok[...]
+    pre[...] = jnp.zeros_like(pre)
+    logit[...] = jnp.zeros_like(logit)
+    for i, g in enumerate((gx, gy, gd)):
+        got(ex.at[g], es.at[i], er.at[i])
+    for i in range(1, 2 * depth):
+        got(ex.at[3 + i], es.at[2 + i], er.at[2 + i])
+    ex[dp] = extra[...]
+    ex[4 + 2 * depth - 1] = extra[...]
+    load_in.wait()
+
+    for s in range(depth):
+        zz = origin(s)
+        got(xs.at[gx, zz, k, top], xs_s.at[s, 0], xs_r.at[s, 0])
+        send(xs.at[gx, zz, k, top], xs.at[gx, zz, k, top], fs.at[s, 0], fr.at[s, 0], (gy, me))
+        got(xs.at[gy, zz, k, low], xs_s.at[s, 1], xs_r.at[s, 1])
+        send(xs.at[gy, zz, k, low], xs.at[gy, zz, k, low], fs.at[s, 1], fr.at[s, 1], (gx, me))
+        if s + 1 < depth:
+            got(xs.at[dp, origin(s + 1), k], zs.at[s + 1], zr.at[s + 1])
+            spread(s + 1)
+        got(xs.at[gx, zz, k, low], xs_s.at[s, 2], xs_r.at[s, 2])
+        send(xs.at[gx, zz, k], xs.at[gx, zz, k], ds.at[s, 1], dr.at[s, 1], (dp, other))
+        got(xs.at[gy, zz, k, top], xs_s.at[s, 3], xs_r.at[s, 3])
+        send(xs.at[gy, zz, k], xs.at[gy, zz, k], ds.at[s, 2], dr.at[s, 2], (dp, other))
+        got(xs.at[gd, zz, k, top], fs.at[s, 0], fr.at[s, 0])
+        got(xs.at[gd, zz, k, low], fs.at[s, 1], fr.at[s, 1])
+        send(xs.at[gd, zz, k], xs.at[gd, zz, k], ds.at[s, 3], dr.at[s, 3], (dp, other))
+        for i, g in enumerate((dp, gx, gy, gd)):
+            got(xs.at[g, zz, 1 - k], ds.at[s, i], dr.at[s, i])
+
+        def gate_of(kk):
+            away = lax.rem(me + 2 * depth - (zz * 2 + kk), 2 * depth)
+            return ex[4 + lax.rem(away + 2 * depth - 1, 2 * depth)]
+
+        gates = [gate_of(kk) for kk in range(2)]
+
+        def accumulate(g, carry):
+            total, score = pre[g], logit[g]
+            for kk in range(2):
+                rows = pl.ds(pl.multiple_of((zz * 2 + kk) * width, width), width)
+                block = xs[g, zz, kk]
+                total += jnp.dot(block, win[rows, :], preferred_element_type=F32)
+                score += lax.dot_general(gates[kk], block, (((1,), (1,)), ((), ())), preferred_element_type=F32)
+            pre[g] = total
+            logit[g] = score
+            return carry
+
+        lax.fori_loop(0, 4, accumulate, 0)
+
+    def activate(g, carry):
+        score = logit[g]
+        row = lax.broadcasted_iota(jnp.int32, score.shape, 0)
+        raised = jnp.where(row < experts, jnp.exp(score), 0.0)
+        chance = raised / jnp.sum(raised, axis=0, keepdims=True)
+        mine = jnp.sum(jnp.where(row == dp, chance, 0.0), axis=0, keepdims=True)
+        picks = ex[g][:, :group].astype(F32)
+        named = jnp.logical_and(jnp.logical_or(row == experts, row == experts + 1), picks == dp.astype(F32))
+        hit = jnp.sum(jnp.where(named, 1.0, 0.0), axis=0, keepdims=True)
+        scale = mine.astype(BF16).astype(F32) * hit
+        column = jnp.transpose(jnp.broadcast_to(scale, (128, group)))[:, :1]
+        acted = jax.nn.gelu(pre[g], approximate=True)
+        hidden[g] = (acted * column).astype(BF16)
+        return carry
+
+    lax.fori_loop(0, 4, activate, 0)
+    load_out.wait()
+
+    def target(s):
+        return lax.rem(z + 1 + s, depth)
+
+    def product(g, zz, kk):
+        cols = pl.ds(pl.multiple_of((zz * 2 + kk) * width, width), width)
+        return jnp.dot(hidden[g], wout[:, cols], preferred_element_type=F32)
+
+    def for_partner(s):
+        def one(g, carry):
+            give[s, g] = product(g, target(s), 1 - k).astype(BF16)
+            return carry
+
+        lax.fori_loop(0, 4, one, 0)
+        send(give.at[s], take.at[s], ps.at[s], pr.at[s], (dp, other))
+
+    def own(s):
+        got(take.at[s], ps.at[s], pr.at[s])
+
+        def one(g, carry):
+            part[s, g] = (product(g, target(s), k) + take[s, g].astype(F32)).astype(BF16)
+            return carry
+
+        lax.fori_loop(0, 4, one, 0)
+
+    def first_hop(s):
+        for i, (g, rows, who) in enumerate(((gd, top, gx), (gd, low, gy), (gx, top, gx), (gy, low, gy))):
+            send(part.at[s, g, rows], hop.at[s, i], hs.at[s, i], hr.at[s, i], (who, me))
+
+    def add(s, g, rows, i):
+        part[s, g, rows] = (part[s, g, rows].astype(F32) + hop[s, i].astype(F32)).astype(BF16)
+
+    def second_hop(s):
+        got(hop.at[s, 0], hs.at[s, 0], hr.at[s, 0])
+        add(s, gy, top, 0)
+        send(part.at[s, gy, top], hop.at[s, 4], hs.at[s, 4], hr.at[s, 4], (gy, me))
+        got(hop.at[s, 1], hs.at[s, 1], hr.at[s, 1])
+        add(s, gx, low, 1)
+        send(part.at[s, gx, low], hop.at[s, 5], hs.at[s, 5], hr.at[s, 5], (gx, me))
+
+    def settle(s):
+        for i in (2, 3, 4, 5):
+            got(hop.at[s, i], hs.at[s, i], hr.at[s, i])
+        for rows, a, b in ((top, 2, 4), (low, 3, 5)):
+            total = part[s, dp, rows].astype(F32) + hop[s, a].astype(F32) + hop[s, b].astype(F32)
+            part[s, dp, rows] = total.astype(BF16)
+        if s + 1 < depth:
+            send(part.at[s, dp], zin.at[s], us.at[s], ur.at[s], (dp, target(s) * 2 + k))
+
+    for_partner(0)
+    for_partner(1)
+    own(0)
+    first_hop(0)
+    for s in range(1, depth):
+        if s + 1 < depth:
+            for_partner(s + 1)
+        own(s)
+        second_hop(s - 1)
+        first_hop(s)
+        if s > 1:
+            settle(s - 2)
+    second_hop(depth - 1)
+    settle(depth - 2)
+    settle(depth - 1)
+    final = part[depth - 1, dp].astype(F32)
+    for s in range(depth - 1):
+        got(zin.at[s], us.at[s], ur.at[s])
+        final += zin[s].astype(F32)
+    out[...] = final.astype(BF16)
+    for copy in started:
+        copy.wait_send()
+
+
+def tokens_plan(tokens, routing, gate_weight, expert_in, expert_out):
+    group, width = tokens.shape
+    nx = lax.axis_size("expert")
+    depth = nx // 2
+    experts = gate_weight.shape[1]
+    model, inner = expert_in.shape[1:]
+    extra = jnp.concatenate(
+        [
+            gate_weight.T,
+            jnp.pad(routing.T.astype(BF16), ((0, 0), (0, width - group))),
+            jnp.zeros((14 - experts, width), BF16),
+        ],
+        axis=0,
+    )
+    half = group // 2
+    vmem = pltpu.VMEM
+    dma = pltpu.SemaphoreType.DMA
+    return pl.pallas_call(
+        functools.partial(whole_kernel, experts),
+        out_shape=jax.ShapeDtypeStruct((group, width), BF16),
+        in_specs=[pl.BlockSpec(memory_space=vmem)] * 2 + [pl.BlockSpec(memory_space=pl.ANY)] * 2,
+        out_specs=pl.BlockSpec(memory_space=vmem),
+        scratch_shapes=[
+            vmem((4, depth, 2, group, width), BF16),
+            vmem((4 + nx, 16, width), BF16),
+            vmem((model, inner), BF16),
+            vmem((inner, model), BF16),
+            vmem((4, group, inner), F32),
+            vmem((4, 16, group), F32),
+            vmem((4, group, inner), BF16),
+            vmem((depth, 4, group, width), BF16),
+            vmem((depth, 4, group, width), BF16),
+            vmem((depth, 4, group, width), BF16),
+            vmem((depth, 6, half, width), BF16),
+            vmem((depth - 1, group, width), BF16),
+            dma((2,)),
+            dma((depth, 4)), dma((depth, 4)),
+            dma((depth,)), dma((depth,)),
+            dma((depth, 2)), dma((depth, 2)),
+            dma((depth, 4)), dma((depth, 4)),
+            dma((2 + nx,)), dma((2 + nx,)),
+            dma((depth,)), dma((depth,)),
+            dma((depth, 6)), dma((depth, 6)),
+            dma((depth - 1,)), dma((depth - 1,)),
+        ],
+        compiler_params=pltpu.CompilerParams(
+            collective_id=0, has_side_effects=True, vmem_limit_bytes=63 * 1024 * 1024
+        ),
+    )(tokens, extra, expert_in, expert_out)
+
+
 def solution(mesh):
     placed = (
         P("dp", "expert"),
@@ -81,6 +332,7 @@
         P("dp", None, "expert"),
         P("dp", "expert", None),
     )
+    body = tokens_plan if mesh.shape["dp"] == 4 else slots_plan
     return jax.shard_map(
-        shards, mesh=mesh, in_specs=placed, out_specs=P("dp", "expert"), check_vma=False
-    )
+        body, mesh=mesh, in_specs=placed, out_specs=P("dp", "expert"), check_vma=False
+    )

time: 208 us -> 125 us (0.60)
  waiting for transfers between devices: 133 us -> 0 us
  Pallas kernels: 0 us -> 121 us
  blocking collectives: 30 us -> 0 us
  matrix products: 24.2 us -> 0 us
  between operations: 13.5 us -> 0.01 us
  starting transfers between devices: 3.69 us -> 0 us
    pallas_call x0 -> x1, Pallas kernels: none -> 121 us  [tokens_plan(): pl.pallas_call(functools.partial(whole_kernel, experts), out_shape=jax.Sh...]
    reduce_scatter x1 -> x0, waiting for transfers between devices: 68.5 us -> none  [expert_rows(): lax.psum_scatter(partial_out.astype(jnp.bfloat16), 'expert', scatter_dime...]
    all_gather x1 -> x0, waiting for transfers between devices: 64.5 us -> none  [expert_rows(): lax.all_gather(flat_rows, 'expert', axis=1, tiled=True)]
    dot_general x4 -> x0, matrix products: 24.2 us -> none  [the longest x1 22.3 us: expert_rows(): jnp.dot(hidden, weight_out, preferred_element_type=jnp.float32)]
    all_to_all x1 -> x0, blocking collectives: 16.4 us -> none  [shards(): lax.all_to_all(outgoing, 'dp', split_axis=0, concat_axis=0, tiled=True)]
    psum x1 -> x0, blocking collectives: 13.6 us -> none  [shards(): logits = lax.psum(partial_logits, 'expert')]
    all_to_all x1 -> x0, starting transfers between devices: 3.65 us -> none  [shards(): lax.all_to_all(processed, 'dp', split_axis=0, concat_axis=0, tiled=True)]
  transfers between devices with their start and end apart: 3 -> 0, of which waited for: 2 -> 0; matrix products, arithmetic and copies ran while one was open for 0% -> 0% of each run, Pallas kernels for 0% -> 0%
where the time goes in v1:
time: 125 us
  Pallas kernels  121 us (97%)
  other arithmetic  2.05 us (2%)
  local copies, waits for them, and re-layouts  1.75 us (1%)
    pallas_call x1, Pallas kernels, tokens_plan(): pl.pallas_call(functools.partial(whole_kernel, experts), out_shape=jax.Sh...  121 us

profile of v1, /device:TPU:0, one launch (start us, length us, event | category | flops | bytes accessed | tf_op | source)
XLA Modules:
  0.0 124.8 jit_solution(8284292063796631396)
XLA Ops:
  0.0 0.1 pad.7.clone
  0.1 0.7 convert_bitcast_fusion
  0.8 1.4 %fusion.3.extra = bf16[16,512]{1,0:T(8,128)(2,1)} fusion(bf16[2,256]{1,0:T(2,128)(2,1)S(1)} %convert_bitcast_fusion, bf16[4,512]{1,0:T(4,128)(2,1)} %bitcast.3, bf16[16]{0:T(256)(128)(2,1)S(1)} %pad.7.clone), kind=kLoop, calls=%fused_computation.5 | loop fusion | flops 81920 | bytes 21536 | tf_op jit(solution)/shard_map/concatenate | solution.py:282
  2.1 121.0 %shard_map.55 = bf16[256,512]{1,0:T(8,128)(2,1)} custom-call(bf16[256,512]{1,0:T(8,128)(2,1)} %tok.1, bf16[16,512]{1,0:T(8,128)(2,1)} %fusion.3.extra, bf16[1,4096,1024]{2,1,0:T(8,128)(2,1)} %win_hbm.1, bf16[1,1024,4096]{2,1,0:T(8,128)(2,1)} %wout_hbm.1), custom_call_target="tpu_custom_call" | custom-call | tf_op jit(solution)/shard_map/pallas_call | solution.py:293
  123.1 1.7 %copy.7 = bf16[256,512]{1,0:T(8,128)(2,1)} copy(bf16[256,512]{1,0:T(8,128)(2,1)} %shard_map.55) | data formatting | bytes 524288
  (1 shorter events, 0.0 us)

commit v2 on v1

--- a/solution.py
+++ b/solution.py
@@ -118,8 +118,24 @@
         pl.semaphore_signal(barrier, inc=1, device_id=who, device_id_type=MESH)
     pl.semaphore_wait(barrier, len(peers))
 
+    upper = z // 2
+    near = z * (1 - upper) + (depth - 1 - z) * upper
+    middle = near == 1
+
     def origin(s):
-        return lax.rem(z + depth - s, depth)
+        seen = near if s == 0 else 1 - near if s == 1 else s
+        return seen * (1 - upper) + (depth - 1 - seen) * upper
+
+    def pass_on(block, b, to, s_sem):
+        return pltpu.make_async_remote_copy(
+            block, xs.at[dp, b, k], s_sem, zr.at[b], device_id=(dp, to * 2 + k), device_id_type=MESH
+        )
+
+    def forward(s):
+        b = origin(s)
+        block = xs.at[dp, b, k]
+        to = jnp.where(b < z, z + 1, z - 1)
+        return pass_on(block, b, to, zs.at[s])
 
     def spread(s):
         zz = origin(s)
@@ -128,8 +144,13 @@
             send(block.at[rows], xs.at[dp, zz, k, rows], xs_s.at[s, i], xs_r.at[s, i], (who, me))
         send(block, xs.at[dp, zz, k], ds.at[s, 0], dr.at[s, 0], (dp, other))
 
-    for i in range(1, depth):
-        send(tok, xs.at[dp, z, k], zs.at[i], zr.at[i], (dp, lax.rem(z + i, depth) * 2 + k))
+    send(tok, xs.at[dp, z, k], zs.at[0], zr.at[z], (dp, (z + 1 - 2 * (z % 2)) * 2 + k))
+    crossing = pass_on(tok, z, depth - 1 - z, zs.at[depth])
+
+    @pl.when(middle)
+    def _():
+        crossing.start()
+
     spread(0)
     for i, who in enumerate(peers):
         slot = dp if i < 3 else 4 + i - 3
@@ -152,7 +173,10 @@
         got(xs.at[gy, zz, k, low], xs_s.at[s, 1], xs_r.at[s, 1])
         send(xs.at[gy, zz, k, low], xs.at[gy, zz, k, low], fs.at[s, 1], fr.at[s, 1], (gx, me))
         if s + 1 < depth:
-            got(xs.at[dp, origin(s + 1), k], zs.at[s + 1], zr.at[s + 1])
+            later = origin(s + 1)
+            got(xs.at[dp, later, k], zs.at[s + 1], zr.at[later])
+            onward = forward(s + 1)
+            pl.when(middle)(onward.start)
             spread(s + 1)
         got(xs.at[gx, zz, k, low], xs_s.at[s, 2], xs_r.at[s, 2])
         send(xs.at[gx, zz, k], xs.at[gx, zz, k], ds.at[s, 1], dr.at[s, 1], (dp, other))
@@ -161,9 +185,6 @@
         got(xs.at[gd, zz, k, top], fs.at[s, 0], fr.at[s, 0])
         got(xs.at[gd, zz, k, low], fs.at[s, 1], fr.at[s, 1])
         send(xs.at[gd, zz, k], xs.at[gd, zz, k], ds.at[s, 3], dr.at[s, 3], (dp, other))
-        for i, g in enumerate((dp, gx, gy, gd)):
-            got(xs.at[g, zz, 1 - k], ds.at[s, i], dr.at[s, i])
-
         def gate_of(kk):
             away = lax.rem(me + 2 * depth - (zz * 2 + kk), 2 * depth)
             return ex[4 + lax.rem(away + 2 * depth - 1, 2 * depth)]
@@ -181,7 +202,10 @@
             logit[g] = score
             return carry
 
-        lax.fori_loop(0, 4, accumulate, 0)
+        if s + 1 < depth:
+            for i, g in enumerate((dp, gx, gy, gd)):
+                got(xs.at[g, zz, 1 - k], ds.at[s, i], dr.at[s, i])
+            lax.fori_loop(0, 4, accumulate, 0)
 
     def activate(g, carry):
         score = logit[g]
@@ -198,7 +222,10 @@
         hidden[g] = (acted * column).astype(BF16)
         return carry
 
-    lax.fori_loop(0, 4, activate, 0)
+    for i, g in enumerate((dp, gx, gy, gd)):
+        got(xs.at[g, zz, 1 - k], ds.at[depth - 1, i], dr.at[depth - 1, i])
+        accumulate(g, 0)
+        activate(g, 0)
     load_out.wait()
 
     def target(s):
@@ -271,6 +298,12 @@
     out[...] = final.astype(BF16)
     for copy in started:
         copy.wait_send()
+
+    @pl.when(middle)
+    def _():
+        crossing.wait_send()
+        for s in range(1, depth):
+            forward(s).wait_send()
 
 
 def tokens_plan(tokens, routing, gate_weight, expert_in, expert_out):
@@ -310,7 +343,7 @@
             vmem((depth - 1, group, width), BF16),
             dma((2,)),
             dma((depth, 4)), dma((depth, 4)),
-            dma((depth,)), dma((depth,)),
+            dma((depth + 1,)), dma((depth,)),
             dma((depth, 2)), dma((depth, 2)),
             dma((depth, 4)), dma((depth, 4)),
             dma((2 + nx,)), dma((2 + nx,)),
@@ -332,7 +365,7 @@
         P("dp", None, "expert"),
         P("dp", "expert", None),
     )
-    body = tokens_plan if mesh.shape["dp"] == 4 else slots_plan
+    body = tokens_plan if tuple(mesh.shape.values()) == (4, 8) else slots_plan
     return jax.shard_map(
         body, mesh=mesh, in_specs=placed, out_specs=P("dp", "expert"), check_vma=False
     )

time: 125 us -> 105 us (0.84)
  Pallas kernels: 121 us -> 101 us
    pallas_call x1, Pallas kernels: 121 us -> 101 us  [tokens_plan(): pl.pallas_call(functools.partial(whole_kernel, experts), out_shape=jax.Sh...]
where the time goes in v2:
time: 105 us
  Pallas kernels  101 us (96%)
  other arithmetic  2.05 us (2%)
  local copies, waits for them, and re-layouts  1.75 us (2%)
    pallas_call x1, Pallas kernels, tokens_plan(): pl.pallas_call(functools.partial(whole_kernel, experts), out_shape=jax.Sh...  101 us

profile of v2, /device:TPU:0, one launch (start us, length us, event | category | flops | bytes accessed | tf_op | source)
XLA Modules:
  0.0 104.6 jit_solution(15018521400223610820)
XLA Ops:
  0.0 0.1 pad.7.clone
  0.1 0.7 convert_bitcast_fusion
  0.8 1.4 %fusion.3.extra = bf16[16,512]{1,0:T(8,128)(2,1)} fusion(bf16[2,256]{1,0:T(2,128)(2,1)S(1)} %convert_bitcast_fusion, bf16[4,512]{1,0:T(4,128)(2,1)} %bitcast.3, bf16[16]{0:T(256)(128)(2,1)S(1)} %pad.7.clone), kind=kLoop, calls=%fused_computation.5 | loop fusion | flops 81920 | bytes 21536 | tf_op jit(solution)/shard_map/concatenate | solution.py:315
  2.1 100.8 %shard_map.55 = bf16[256,512]{1,0:T(8,128)(2,1)} custom-call(bf16[256,512]{1,0:T(8,128)(2,1)} %tok.1, bf16[16,512]{1,0:T(8,128)(2,1)} %fusion.3.extra, bf16[1,4096,1024]{2,1,0:T(8,128)(2,1)} %win_hbm.1, bf16[1,1024,4096]{2,1,0:T(8,128)(2,1)} %wout_hbm.1), custom_call_target="tpu_custom_call" | custom-call | tf_op jit(solution)/shard_map/pallas_call | solution.py:326
  102.9 1.7 %copy.7 = bf16[256,512]{1,0:T(8,128)(2,1)} copy(bf16[256,512]{1,0:T(8,128)(2,1)} %shard_map.55) | data formatting | bytes 524288
  (1 shorter events, 0.0 us)

commit v3 on v2

--- a/solution.py
+++ b/solution.py
@@ -84,7 +84,8 @@
 
 def whole_kernel(
     experts,
-    tok, extra, win_hbm, wout_hbm, out,
+    tok, gate_in, routes, win_hbm, wout_hbm, out,
+    extra,
     xs, ex, win, wout, pre, logit, hidden, give, take, part, hop, zin,
     wsem, xs_s, xs_r, zs, zr, fs, fr, ds, dr, es, er, ps, pr, hs, hr, us, ur,
 ):
@@ -152,6 +153,17 @@
         crossing.start()
 
     spread(0)
+    wide = lax.broadcasted_iota(jnp.int32, (16, experts), 0) == lax.broadcasted_iota(jnp.int32, (16, experts), 1)
+    pair = lax.broadcasted_iota(jnp.int32, (16, 2), 0) == lax.broadcasted_iota(jnp.int32, (16, 2), 1) + experts
+    across = (((1,), (1,)), ((), ()))
+    gate_rows = lax.dot_general(
+        jnp.where(wide, 1.0, 0.0).astype(BF16), gate_in[...], across, preferred_element_type=F32
+    )
+    route_rows = lax.dot_general(
+        jnp.where(pair, 1.0, 0.0).astype(BF16), routes[...].astype(F32).astype(BF16), across, preferred_element_type=F32
+    )
+    extra[...] = gate_rows.astype(BF16)
+    extra[:, :group] = (gate_rows[:, :group] + route_rows).astype(BF16)
     for i, who in enumerate(peers):
         slot = dp if i < 3 else 4 + i - 3
         send(extra, ex.at[slot], es.at[i], er.at[i], who)
@@ -166,6 +178,31 @@
     ex[4 + 2 * depth - 1] = extra[...]
     load_in.wait()
 
+    def along(s):
+        b = origin(s)
+        got(xs.at[dp, b, k], zs.at[s], zr.at[b])
+
+    def relay(s):
+        pl.when(middle)(forward(s).start)
+
+    def accumulate(s, g):
+        zz = origin(s)
+        total, score = pre[g], logit[g]
+        for kk in range(2):
+            away = lax.rem(me + 2 * depth - (zz * 2 + kk), 2 * depth)
+            gate = ex[4 + lax.rem(away + 2 * depth - 1, 2 * depth)]
+            rows = pl.ds(pl.multiple_of((zz * 2 + kk) * width, width), width)
+            block = xs[g, zz, kk]
+            total += jnp.dot(block, win[rows, :], preferred_element_type=F32)
+            score += lax.dot_general(gate, block, (((1,), (1,)), ((), ())), preferred_element_type=F32)
+        pre[g] = total
+        logit[g] = score
+
+    def absorb(s):
+        for i, g in enumerate((dp, gx, gy, gd)):
+            got(xs.at[g, origin(s), 1 - k], ds.at[s, i], dr.at[s, i])
+        lax.fori_loop(0, 4, lambda g, carry: accumulate(s, g) or carry, 0)
+
     for s in range(depth):
         zz = origin(s)
         got(xs.at[gx, zz, k, top], xs_s.at[s, 0], xs_r.at[s, 0])
@@ -173,11 +210,19 @@
         got(xs.at[gy, zz, k, low], xs_s.at[s, 1], xs_r.at[s, 1])
         send(xs.at[gy, zz, k, low], xs.at[gy, zz, k, low], fs.at[s, 1], fr.at[s, 1], (gx, me))
         if s + 1 < depth:
-            later = origin(s + 1)
-            got(xs.at[dp, later, k], zs.at[s + 1], zr.at[later])
-            onward = forward(s + 1)
-            pl.when(middle)(onward.start)
+            if s == 0:
+                along(1)
+                relay(1)
+                pl.when(middle)(lambda: along(2))
+                relay(2)
+            else:
+                pl.when(jnp.logical_not(middle))(functools.partial(along, s + 1))
+            if s == 1:
+                pl.when(middle)(lambda: along(3))
+                relay(3)
             spread(s + 1)
+        if s > 0:
+            absorb(s - 1)
         got(xs.at[gx, zz, k, low], xs_s.at[s, 2], xs_r.at[s, 2])
         send(xs.at[gx, zz, k], xs.at[gx, zz, k], ds.at[s, 1], dr.at[s, 1], (dp, other))
         got(xs.at[gy, zz, k, top], xs_s.at[s, 3], xs_r.at[s, 3])
@@ -185,27 +230,6 @@
         got(xs.at[gd, zz, k, top], fs.at[s, 0], fr.at[s, 0])
         got(xs.at[gd, zz, k, low], fs.at[s, 1], fr.at[s, 1])
         send(xs.at[gd, zz, k], xs.at[gd, zz, k], ds.at[s, 3], dr.at[s, 3], (dp, other))
-        def gate_of(kk):
-            away = lax.rem(me + 2 * depth - (zz * 2 + kk), 2 * depth)
-            return ex[4 + lax.rem(away + 2 * depth - 1, 2 * depth)]
-
-        gates = [gate_of(kk) for kk in range(2)]
-
-        def accumulate(g, carry):
-            total, score = pre[g], logit[g]
-            for kk in range(2):
-                rows = pl.ds(pl.multiple_of((zz * 2 + kk) * width, width), width)
-                block = xs[g, zz, kk]
-                total += jnp.dot(block, win[rows, :], preferred_element_type=F32)
-                score += lax.dot_general(gates[kk], block, (((1,), (1,)), ((), ())), preferred_element_type=F32)
-            pre[g] = total
-            logit[g] = score
-            return carry
-
-        if s + 1 < depth:
-            for i, g in enumerate((dp, gx, gy, gd)):
-                got(xs.at[g, zz, 1 - k], ds.at[s, i], dr.at[s, i])
-            lax.fori_loop(0, 4, accumulate, 0)
 
     def activate(g, carry):
         score = logit[g]
@@ -222,39 +246,32 @@
         hidden[g] = (acted * column).astype(BF16)
         return carry
 
-    for i, g in enumerate((dp, gx, gy, gd)):
-        got(xs.at[g, zz, 1 - k], ds.at[depth - 1, i], dr.at[depth - 1, i])
-        accumulate(g, 0)
-        activate(g, 0)
-    load_out.wait()
-
     def target(s):
-        return lax.rem(z + 1 + s, depth)
+        return origin(depth - 1 - s)
 
     def product(g, zz, kk):
         cols = pl.ds(pl.multiple_of((zz * 2 + kk) * width, width), width)
         return jnp.dot(hidden[g], wout[:, cols], preferred_element_type=F32)
 
+    def lend(s, g):
+        give[s, g] = product(g, target(s), 1 - k).astype(BF16)
+
+    def keep(s, g):
+        part[s, g] = (product(g, target(s), k) + take[s, g].astype(F32)).astype(BF16)
+
     def for_partner(s):
-        def one(g, carry):
-            give[s, g] = product(g, target(s), 1 - k).astype(BF16)
-            return carry
-
-        lax.fori_loop(0, 4, one, 0)
-        send(give.at[s], take.at[s], ps.at[s], pr.at[s], (dp, other))
+        lax.fori_loop(0, 4, lambda g, carry: lend(s, g) or carry, 0)
+        send(give.at[s], take.at[s], ps.at[s, 0], pr.at[s, 0], (dp, other))
 
     def own(s):
-        got(take.at[s], ps.at[s], pr.at[s])
-
-        def one(g, carry):
-            part[s, g] = (product(g, target(s), k) + take[s, g].astype(F32)).astype(BF16)
-            return carry
-
-        lax.fori_loop(0, 4, one, 0)
-
-    def first_hop(s):
-        for i, (g, rows, who) in enumerate(((gd, top, gx), (gd, low, gy), (gx, top, gx), (gy, low, gy))):
-            send(part.at[s, g, rows], hop.at[s, i], hs.at[s, i], hr.at[s, i], (who, me))
+        got(take.at[s], ps.at[s, 0], pr.at[s, 0])
+        lax.fori_loop(0, 4, lambda g, carry: keep(s, g) or carry, 0)
+
+    hops = ((gd, top, gx), (gd, low, gy), (gx, top, gx), (gy, low, gy))
+
+    def leave(s, i):
+        g, rows, who = hops[i]
+        send(part.at[s, g, rows], hop.at[s, i], hs.at[s, i], hr.at[s, i], (who, me))
 
     def add(s, g, rows, i):
         part[s, g, rows] = (part[s, g, rows].astype(F32) + hop[s, i].astype(F32)).astype(BF16)
@@ -267,35 +284,82 @@
         add(s, gx, low, 1)
         send(part.at[s, gx, low], hop.at[s, 5], hs.at[s, 5], hr.at[s, 5], (gx, me))
 
+    outer = z + 1 - 2 * (z % 2)
+    last = depth - 1
+
+    def line(s):
+        far = jnp.where(middle, depth - 1 - z, outer) if s < 2 else outer
+        slot = jnp.where(middle, last + s, s)
+        return pltpu.make_async_remote_copy(
+            part.at[s, dp], zin.at[slot], us.at[s], ur.at[slot], device_id=(dp, far * 2 + k), device_id_type=MESH
+        )
+
     def settle(s):
         for i in (2, 3, 4, 5):
             got(hop.at[s, i], hs.at[s, i], hr.at[s, i])
         for rows, a, b in ((top, 2, 4), (low, 3, 5)):
             total = part[s, dp, rows].astype(F32) + hop[s, a].astype(F32) + hop[s, b].astype(F32)
             part[s, dp, rows] = total.astype(BF16)
-        if s + 1 < depth:
-            send(part.at[s, dp], zin.at[s], us.at[s], ur.at[s], (dp, target(s) * 2 + k))
-
-    for_partner(0)
+        if s < last:
+            pl.when(jnp.logical_not(middle))(line(s).start)
+
+    def gather_in(slot):
+        got(zin.at[slot], us.at[0], ur.at[slot])
+        return zin[slot].astype(F32)
+
+    def merge(s):
+        @pl.when(middle)
+        def _():
+            came = gather_in(s if s < 2 else last)
+            part[s, dp] = (part[s, dp].astype(F32) + came).astype(BF16)
+            line(s).start()
+
+    load_out.wait()
+    for i, g in enumerate((dp, gx, gy, gd)):
+        got(xs.at[g, zz, 1 - k], ds.at[last, i], dr.at[last, i])
+        accumulate(last, g)
+        activate(g, 0)
+        lend(0, g)
+        send(give.at[0, g], take.at[0, g], ps.at[0, i], pr.at[0, i], (dp, other))
+    for i, g, ways in ((1, gx, (2,)), (2, gy, (3,)), (3, gd, (0, 1)), (0, dp, ())):
+        got(take.at[0, g], ps.at[0, i], pr.at[0, i])
+        keep(0, g)
+        for way in ways:
+            leave(0, way)
     for_partner(1)
-    own(0)
-    first_hop(0)
-    for s in range(1, depth):
-        if s + 1 < depth:
-            for_partner(s + 1)
-        own(s)
-        second_hop(s - 1)
-        first_hop(s)
+    own(1)
+    leave(1, 0)
+    leave(1, 1)
+    for_partner(2)
+    for s in range(depth):
+        second_hop(s)
+        if s < last:
+            leave(s + 1, 2)
+            leave(s + 1, 3)
+        if s + 2 < depth:
+            own(s + 2)
+            leave(s + 2, 0)
+            leave(s + 2, 1)
+        if s + 3 < depth:
+            for_partner(s + 3)
         if s > 1:
-            settle(s - 2)
-    second_hop(depth - 1)
-    settle(depth - 2)
-    settle(depth - 1)
-    final = part[depth - 1, dp].astype(F32)
-    for s in range(depth - 1):
-        got(zin.at[s], us.at[s], ur.at[s])
-        final += zin[s].astype(F32)
-    out[...] = final.astype(BF16)
+            merge(s - 2)
+        if s > 0:
+            settle(s - 1)
+    merge(last - 1)
+    settle(last)
+
+    @pl.when(middle)
+    def _():
+        final = part[last, dp].astype(F32) + gather_in(2) + gather_in(last + 1)
+        out[...] = final.astype(BF16)
+
+    @pl.when(jnp.logical_not(middle))
+    def _():
+        out[...] = (part[last, dp].astype(F32) + gather_in(last + 2)).astype(BF16)
+
+    for s in range(last):
+        line(s).wait_send()
     for copy in started:
         copy.wait_send()
 
@@ -312,23 +376,16 @@
     depth = nx // 2
     experts = gate_weight.shape[1]
     model, inner = expert_in.shape[1:]
-    extra = jnp.concatenate(
-        [
-            gate_weight.T,
-            jnp.pad(routing.T.astype(BF16), ((0, 0), (0, width - group))),
-            jnp.zeros((14 - experts, width), BF16),
-        ],
-        axis=0,
-    )
     half = group // 2
     vmem = pltpu.VMEM
     dma = pltpu.SemaphoreType.DMA
     return pl.pallas_call(
         functools.partial(whole_kernel, experts),
         out_shape=jax.ShapeDtypeStruct((group, width), BF16),
-        in_specs=[pl.BlockSpec(memory_space=vmem)] * 2 + [pl.BlockSpec(memory_space=pl.ANY)] * 2,
+        in_specs=[pl.BlockSpec(memory_space=vmem)] * 3 + [pl.BlockSpec(memory_space=pl.ANY)] * 2,
         out_specs=pl.BlockSpec(memory_space=vmem),
         scratch_shapes=[
+            vmem((16, width), BF16),
             vmem((4, depth, 2, group, width), BF16),
             vmem((4 + nx, 16, width), BF16),
             vmem((model, inner), BF16),
@@ -340,21 +397,21 @@
             vmem((depth, 4, group, width), BF16),
             vmem((depth, 4, group, width), BF16),
             vmem((depth, 6, half, width), BF16),
-            vmem((depth - 1, group, width), BF16),
+            vmem((depth + 2, group, width), BF16),
             dma((2,)),
             dma((depth, 4)), dma((depth, 4)),
             dma((depth + 1,)), dma((depth,)),
             dma((depth, 2)), dma((depth, 2)),
             dma((depth, 4)), dma((depth, 4)),
             dma((2 + nx,)), dma((2 + nx,)),
-            dma((depth,)), dma((depth,)),
+            dma((depth, 4)), dma((depth, 4)),
             dma((depth, 6)), dma((depth, 6)),
-            dma((depth - 1,)), dma((depth - 1,)),
+            dma((depth - 1,)), dma((depth + 2,)),
         ],
         compiler_params=pltpu.CompilerParams(
             collective_id=0, has_side_effects=True, vmem_limit_bytes=63 * 1024 * 1024
         ),
-    )(tokens, extra, expert_in, expert_out)
+    )(tokens, gate_weight, routing, expert_in, expert_out)
 
 
 def solution(mesh):

time: 105 us -> 100 us (0.952)
  Pallas kernels: 101 us -> 95.3 us
  local copies, waits for them, and re-layouts: 1.75 us -> 4.64 us
  other arithmetic: 2.05 us -> 0 us
    pallas_call x1, Pallas kernels: 101 us -> 95.3 us  [tokens_plan(): pl.pallas_call(functools.partial(whole_kernel, experts), out_shape=jax.Sh...]
    unnamed x1 -> x3, local copies, waits for them, and re-layouts: 1.67 us -> 4.64 us
    concatenate x1 -> x0, other arithmetic: 1.36 us -> none  [tokens_plan(): jnp.concatenate([gate_weight.T, jnp.pad(routing.T.astype(BF16), ((0, 0),...]
where the time goes in v3:
time: 100 us; the launch traced here: 99.9 us
  Pallas kernels  95.3 us (95%)
  local copies, waits for them, and re-layouts  4.64 us (5%)
    pallas_call x1, Pallas kernels, tokens_plan(): pl.pallas_call(functools.partial(whole_kernel, experts), out_shape=jax.Sh...  95.3 us
    unnamed x3, local copies, waits for them, and re-layouts  4.64 us

profile of v3, /device:TPU:0, one launch (start us, length us, event | category | flops | bytes accessed | tf_op | source)
XLA Modules:
  0.0 99.9 jit_solution(11120319772429691277)
XLA Ops:
  0.0 1.5 %copy.7.routes = s32[256,2]{1,0:T(8,128)} copy(s32[256,2]{0,1:T(2,128)} %param.6) | data formatting | bytes 4096 | tf_op args[1]
  1.5 1.5 %copy.6.gate_in = bf16[512,4]{1,0:T(8,128)(2,1)} copy(bf16[512,4]{0,1:T(4,128)(2,1)} %param.7) | data formatting | bytes 8192 | tf_op args[2]
  3.0 95.3 %shard_map.55 = bf16[256,512]{1,0:T(8,128)(2,1)} custom-call(bf16[256,512]{1,0:T(8,128)(2,1)} %tok.1, bf16[512,4]{1,0:T(8,128)(2,1)} %copy.6.gate_in, s32[256,2]{1,0:T(8,128)} %copy.7.routes, bf16[1,4096,1024]{2,1,0:T(8,128)(2,1)} %win_hbm.1, bf16[1,1024,4096]{2,1,0:T(8,128)(2,1)} %wout_hbm.1), custom_call_target="tpu_custom_call" | custom-call | tf_op jit(solution)/shard_map/pallas_call | solution.py:382
  98.3 1.7 %copy.9 = bf16[256,512]{1,0:T(8,128)(2,1)} copy(bf16[256,512]{1,0:T(8,128)(2,1)} %shard_map.55) | data formatting | bytes 524288

commit v4 on v3

--- a/solution.py
+++ b/solution.py
@@ -170,13 +170,6 @@
     xs[dp, z, k] = tok[...]
     pre[...] = jnp.zeros_like(pre)
     logit[...] = jnp.zeros_like(logit)
-    for i, g in enumerate((gx, gy, gd)):
-        got(ex.at[g], es.at[i], er.at[i])
-    for i in range(1, 2 * depth):
-        got(ex.at[3 + i], es.at[2 + i], er.at[2 + i])
-    ex[dp] = extra[...]
-    ex[4 + 2 * depth - 1] = extra[...]
-    load_in.wait()
 
     def along(s):
         b = origin(s)
@@ -221,6 +214,14 @@
                 pl.when(middle)(lambda: along(3))
                 relay(3)
             spread(s + 1)
+        if s == 1:
+            for i, g in enumerate((gx, gy, gd)):
+                got(ex.at[g], es.at[i], er.at[i])
+            for i in range(1, 2 * depth):
+                got(ex.at[3 + i], es.at[2 + i], er.at[2 + i])
+            ex[dp] = extra[...]
+            ex[4 + 2 * depth - 1] = extra[...]
+            load_in.wait()
         if s > 0:
             absorb(s - 1)
         got(xs.at[gx, zz, k, low], xs_s.at[s, 2], xs_r.at[s, 2])

time: 100 us -> 96.3 us (0.963)
  Pallas kernels: 95.3 us -> 91.5 us
    pallas_call x1, Pallas kernels: 95.3 us -> 91.5 us  [tokens_plan(): pl.pallas_call(functools.partial(whole_kernel, experts), out_shape=jax.Sh...]
where the time goes in v4:
time: 96.3 us; the launch traced here: 96.1 us
  Pallas kernels  91.5 us (95%)
  local copies, waits for them, and re-layouts  4.64 us (5%)
    pallas_call x1, Pallas kernels, tokens_plan(): pl.pallas_call(functools.partial(whole_kernel, experts), out_shape=jax.Sh...  91.5 us
    unnamed x3, local copies, waits for them, and re-layouts  4.64 us

profile of v4, /device:TPU:0, one launch (start us, length us, event | category | flops | bytes accessed | tf_op | source)
XLA Modules:
  0.0 96.1 jit_solution(17522391401533555969)
XLA Ops:
  0.0 1.5 %copy.7.routes = s32[256,2]{1,0:T(8,128)} copy(s32[256,2]{0,1:T(2,128)} %param.6) | data formatting | bytes 4096 | tf_op args[1]
  1.5 1.5 %copy.6.gate_in = bf16[512,4]{1,0:T(8,128)(2,1)} copy(bf16[512,4]{0,1:T(4,128)(2,1)} %param.7) | data formatting | bytes 8192 | tf_op args[2]
  3.0 91.5 %shard_map.55 = bf16[256,512]{1,0:T(8,128)(2,1)} custom-call(bf16[256,512]{1,0:T(8,128)(2,1)} %tok.1, bf16[512,4]{1,0:T(8,128)(2,1)} %copy.6.gate_in, s32[256,2]{1,0:T(8,128)} %copy.7.routes, bf16[1,4096,1024]{2,1,0:T(8,128)(2,1)} %win_hbm.1, bf16[1,1024,4096]{2,1,0:T(8,128)(2,1)} %wout_hbm.1), custom_call_target="tpu_custom_call" | custom-call | tf_op jit(solution)/shard_map/pallas_call | solution.py:383
  94.4 1.7 %copy.9 = bf16[256,512]{1,0:T(8,128)(2,1)} copy(bf16[256,512]{1,0:T(8,128)(2,1)} %shard_map.55) | data formatting | bytes 524288
